TPU v7x, 8 devices: a whole 2x2x1 slice. The times are simulated.
8 devices in a mesh: data: 2 (over z, y), time: 4 (over x, core).
Axes of the slice: x: 2, y: 2, z: 1, core: 2. Of those that a mesh axis runs over, the one named last changes fastest.
Arguments:
- x_init: float32 [128, 256, 16], P('data'), parts along dimension 0
- w_in: bfloat16 [16, 1152], replicated
- w_out: bfloat16 [1152, 16], replicated
- mod_scale: bfloat16 [4, 1152], P('time')
- mod_shift: bfloat16 [4, 1152], P('time')
- step_size: float32 [4], P('time')
Outputs:
- output: float32 [4, 128, 256, 16], P('time', 'data'), parts along dimension 1
There are 2 independent parts. A program takes and returns all parts, laid end to end along the dimension named above; an argument that names none is the same for every part.
All inputs are finite; a program needn't handle non-finite values.
Results may differ from a plain program's by a relative error of at most 0.001.
Values are sent between devices in bfloat16 or wider.
A program may use at most 1 GiB of HBM per device.

v0:
```python
import jax
import jax.numpy as jnp
from jax import lax
from jax.sharding import PartitionSpec as P

SWEEPS = 4


def drift_block(pre_act, scale, shift, w_out):
    hidden_act = jax.nn.gelu(pre_act * scale + shift, approximate=True)
    return jnp.einsum("kbnd,dc->kbnc", hidden_act.astype(jnp.bfloat16), w_out, preferred_element_type=jnp.float32)


def solution(mesh):
    n_time = mesh.shape["time"]
    from_next = [(source, source - 1) for source in range(1, n_time)]
    hop_dists = [2 ** power for power in range(n_time) if 2 ** power < n_time]

    def local(x_init, w_in, w_out, mod_scale, mod_shift, step_size):
        scale = (1.0 + mod_scale.astype(jnp.float32))[:, None, None, :]
        shift = mod_shift.astype(jnp.float32)[:, None, None, :]
        pre_act = jnp.einsum("bnc,cd->bnd", x_init.astype(jnp.bfloat16), w_in, preferred_element_type=jnp.float32)[None]
        latents = None
        for sweep in range(SWEEPS):
            if sweep > 0:
                pre_act = jnp.einsum("kbnc,cd->kbnd", latents.astype(jnp.bfloat16), w_in, preferred_element_type=jnp.float32)
            drifts = drift_block(pre_act, scale, shift, w_out)
            next_first = lax.ppermute(drifts[0], "time", from_next)
            next_drifts = jnp.concatenate([drifts[1:], next_first[None]], axis=0)
            increments = step_size[:, None, None, None] * (0.5 * (drifts + next_drifts))
            local_cum = jnp.cumsum(increments, axis=0)
            local_excl = jnp.concatenate([jnp.zeros_like(local_cum[:1]), local_cum[:-1]], axis=0)
            dev_total = local_cum[-1]
            inclusive = dev_total
            for distance in hop_dists:
                inclusive = inclusive + lax.ppermute(inclusive, "time", [(source, source + distance) for source in range(n_time - distance)])
            offset = inclusive - dev_total
            latents = x_init[None] + (offset[None] + local_excl)
        return latents

    return jax.shard_map(local, mesh=mesh, in_specs=(P("data"), P(), P(), P("time"), P("time"), P("time")), out_specs=P("time", "data"), check_vma=False)
```

profile of v0, /device:TPU:0, one launch (start us, length us, event | category | flops | bytes accessed | tf_op | source)
XLA Modules:
  0.0 364.2 jit_solution(6730739445978572434)
XLA Ops:
  0.0 0.0 copy-start
  0.0 0.7 convert_reduce_fusion
  0.8 0.0 copy-done
  0.8 33.4 %fusion.35 = f32[64,256,16]{1,2,0:T(8,128)S(1)} fusion(f32[1152]{0:T(1024)S(1)} %get-tuple-element.5, f32[1152]{0:T(1024)S(1)} %get-tuple-element.6, f32[64,256,16]{1,2,0:T(8,128)} %param.6, bf16[1152,16]{0,1:T(8,128)(2,1)S(1)} %copy-done, bf16[16,1152]{1,0:T(8,128)(2,1)} %param.7), kind=kOutput, calls=%fused_computation.39 | convolution fusion | flops 1415839744 | bytes 2180096 | tf_op jit(solution)/shard_map/kbnd,dc->kbnc/dot_general | solution.py:11
  34.2 1.3 collective-permute-start
  36.2 3.0 collective-permute-done
  39.1 0.2 add_multiply_fusion.3
  39.4 0.0 copy-start.1
  39.4 0.0 copy-start.2
  39.4 15.0 %collective-permute-start.1 = (f32[64,256,16]{1,2,0:T(8,128)S(1)}, f32[64,256,16]{1,2,0:T(8,128)S(1)}, u32[]{:S(2)}, u32[]{:S(2)}) collective-permute-start(f32[64,256,16]{1,2,0:T(8,128)S(1)} %add_multiply_fusion.3), channel_id=1, source_target_pairs={{0,1},{1,2},{2,3},{4,5},{5,6},{6,7}} | collective-permute-start | bytes 3145736 | tf_op jit(solution)/shard_map/ppermute | solution.py:36
  54.4 2.2 collective-permute-done.1
  56.6 0.2 add.147
  56.8 14.7 %collective-permute-start.2 = (f32[64,256,16]{1,2,0:T(8,128)S(1)}, f32[64,256,16]{1,2,0:T(8,128)}, u32[]{:S(2)}, u32[]{:S(2)}) collective-permute-start(f32[64,256,16]{1,2,0:T(8,128)S(1)} %add.147), channel_id=1, source_target_pairs={{0,2},{1,3},{4,6},{5,7}} | collective-permute-start | bytes 3145736 | tf_op jit(solution)/shard_map/ppermute | solution.py:36
  71.6 18.8 %collective-permute-done.2 = f32[64,256,16]{1,2,0:T(8,128)} collective-permute-done((f32[64,256,16]{1,2,0:T(8,128)S(1)}, f32[64,256,16]{1,2,0:T(8,128)}, u32[]{:S(2)}, u32[]{:S(2)}) %collective-permute-start.2) | collective-permute-done | bytes 1048608 | tf_op jit(solution)/shard_map/ppermute | solution.py:36
  90.4 0.0 copy-done.1
  90.4 0.0 copy-done.2
  90.4 34.3 %fusion.34 = f32[64,256,16]{1,2,0:T(8,128)} fusion(f32[1152]{0:T(1024)S(1)} %get-tuple-element.5, f32[1152]{0:T(1024)S(1)} %get-tuple-element.6, f32[64,256,16]{1,2,0:T(8,128)S(1)} %copy-done.1, f32[64,256,16]{1,2,0:T(8,128)S(1)} %add_multiply_fusion.3, f32[64,256,16]{1,2,0:T(8,128)S(1)} %add.147, f32[64,256,16]{1,2,0:T(8,128)} %collective-permute-done.2, ...), kind=kOutput, calls=%fused_computation.38 | convolution fusion | flops 1416626176 | bytes 5325824 | tf_op jit(solution)/shard_map/kbnd,dc->kbnc/dot_general | solution.py:11
  124.8 1.3 collective-permute-start.3
  126.1 3.3 collective-permute-done.3
  129.3 1.5 add_multiply_fusion.2
  130.8 14.4 %collective-permute-start.4 = (f32[64,256,16]{1,2,0:T(8,128)S(1)}, f32[64,256,16]{1,2,0:T(8,128)S(1)}, u32[]{:S(2)}, u32[]{:S(2)}) collective-permute-start(f32[64,256,16]{1,2,0:T(8,128)S(1)} %add_multiply_fusion.2), channel_id=1, source_target_pairs={{0,1},{1,2},{2,3},{4,5},{5,6},{6,7}} | collective-permute-start | bytes 3145736 | tf_op jit(solution)/shard_map/ppermute | solution.py:36
  145.2 2.2 collective-permute-done.4
  147.4 0.2 add.154
  147.6 14.7 %collective-permute-start.5 = (f32[64,256,16]{1,2,0:T(8,128)S(1)}, f32[64,256,16]{1,2,0:T(8,128)}, u32[]{:S(2)}, u32[]{:S(2)}) collective-permute-start(f32[64,256,16]{1,2,0:T(8,128)S(1)} %add.154), channel_id=1, source_target_pairs={{0,2},{1,3},{4,6},{5,7}} | collective-permute-start | bytes 3145736 | tf_op jit(solution)/shard_map/ppermute | solution.py:36
  162.4 18.8 %collective-permute-done.5 = f32[64,256,16]{1,2,0:T(8,128)} collective-permute-done((f32[64,256,16]{1,2,0:T(8,128)S(1)}, f32[64,256,16]{1,2,0:T(8,128)}, u32[]{:S(2)}, u32[]{:S(2)}) %collective-permute-start.5) | collective-permute-done | bytes 1048608 | tf_op jit(solution)/shard_map/ppermute | solution.py:36
  181.2 34.3 %fusion.33 = f32[64,256,16]{1,2,0:T(8,128)} fusion(f32[1152]{0:T(1024)S(1)} %get-tuple-element.5, f32[1152]{0:T(1024)S(1)} %get-tuple-element.6, f32[64,256,16]{1,2,0:T(8,128)S(1)} %copy-done.1, f32[64,256,16]{1,2,0:T(8,128)S(1)} %add_multiply_fusion.2, f32[64,256,16]{1,2,0:T(8,128)S(1)} %add.154, f32[64,256,16]{1,2,0:T(8,128)} %collective-permute-done.5, ...), kind=kOutput, calls=%fused_computation.37 | convolution fusion | flops 1416626176 | bytes 5325824 | tf_op jit(solution)/shard_map/kbnd,dc->kbnc/dot_general | solution.py:11
  215.5 1.3 collective-permute-start.6
  216.8 3.3 collective-permute-done.6
  220.1 1.5 add_multiply_fusion.1
  221.6 14.4 %collective-permute-start.7 = (f32[64,256,16]{1,2,0:T(8,128)S(1)}, f32[64,256,16]{1,2,0:T(8,128)S(1)}, u32[]{:S(2)}, u32[]{:S(2)}) collective-permute-start(f32[64,256,16]{1,2,0:T(8,128)S(1)} %add_multiply_fusion.1), channel_id=1, source_target_pairs={{0,1},{1,2},{2,3},{4,5},{5,6},{6,7}} | collective-permute-start | bytes 3145736 | tf_op jit(solution)/shard_map/ppermute | solution.py:36
  236.0 2.2 collective-permute-done.7
  238.2 0.2 add.161
  238.4 14.7 %collective-permute-start.8 = (f32[64,256,16]{1,2,0:T(8,128)S(1)}, f32[64,256,16]{1,2,0:T(8,128)}, u32[]{:S(2)}, u32[]{:S(2)}) collective-permute-start(f32[64,256,16]{1,2,0:T(8,128)S(1)} %add.161), channel_id=1, source_target_pairs={{0,2},{1,3},{4,6},{5,7}} | collective-permute-start | bytes 3145736 | tf_op jit(solution)/shard_map/ppermute | solution.py:36
  253.1 18.8 %collective-permute-done.8 = f32[64,256,16]{1,2,0:T(8,128)} collective-permute-done((f32[64,256,16]{1,2,0:T(8,128)S(1)}, f32[64,256,16]{1,2,0:T(8,128)}, u32[]{:S(2)}, u32[]{:S(2)}) %collective-permute-start.8) | collective-permute-done | bytes 1048608 | tf_op jit(solution)/shard_map/ppermute | solution.py:36
  272.0 34.3 %fusion.32 = f32[64,256,16]{1,2,0:T(8,128)} fusion(f32[1152]{0:T(1024)S(1)} %get-tuple-element.5, f32[1152]{0:T(1024)S(1)} %get-tuple-element.6, f32[64,256,16]{1,2,0:T(8,128)S(1)} %copy-done.1, f32[64,256,16]{1,2,0:T(8,128)S(1)} %add_multiply_fusion.1, f32[64,256,16]{1,2,0:T(8,128)S(1)} %add.161, f32[64,256,16]{1,2,0:T(8,128)} %collective-permute-done.8, ...), kind=kOutput, calls=%fused_computation.36 | convolution fusion | flops 1416626176 | bytes 5325824 | tf_op jit(solution)/shard_map/kbnd,dc->kbnc/dot_general | solution.py:11
  306.3 1.3 collective-permute-start.9
  307.6 3.3 collective-permute-done.9
  310.8 1.5 add_multiply_fusion
  312.3 14.4 %collective-permute-start.10 = (f32[64,256,16]{1,2,0:T(8,128)S(1)}, f32[64,256,16]{1,2,0:T(8,128)S(1)}, u32[]{:S(2)}, u32[]{:S(2)}) collective-permute-start(f32[64,256,16]{1,2,0:T(8,128)S(1)} %add_multiply_fusion), channel_id=1, source_target_pairs={{0,1},{1,2},{2,3},{4,5},{5,6},{6,7}} | collective-permute-start | bytes 3145736 | tf_op jit(solution)/shard_map/ppermute | solution.py:36
  326.7 2.2 collective-permute-done.10
  328.9 0.2 add.168
  329.2 13.8 %collective-permute-start.11 = (f32[64,256,16]{1,2,0:T(8,128)S(1)}, f32[64,256,16]{1,2,0:T(8,128)S(1)}, u32[]{:S(2)}, u32[]{:S(2)}) collective-permute-start(f32[64,256,16]{1,2,0:T(8,128)S(1)} %add.168), channel_id=1, source_target_pairs={{0,2},{1,3},{4,6},{5,7}} | collective-permute-start | bytes 3145736 | tf_op jit(solution)/shard_map/ppermute | solution.py:36
  343.0 19.8 %collective-permute-done.11 = f32[64,256,16]{1,2,0:T(8,128)S(1)} collective-permute-done((f32[64,256,16]{1,2,0:T(8,128)S(1)}, f32[64,256,16]{1,2,0:T(8,128)S(1)}, u32[]{:S(2)}, u32[]{:S(2)}) %collective-permute-start.11) | collective-permute-done | bytes 1048608 | tf_op jit(solution)/shard_map/ppermute | solution.py:36
  362.7 1.5 add_bitcast_fusion
Async XLA Ops:
  0.0 0.8 copy-start
  34.2 4.9 %collective-permute-start = (f32[64,256,16]{1,2,0:T(8,128)S(1)}, f32[64,256,16]{1,2,0:T(8,128)S(1)}, u32[]{:S(2)}, u32[]{:S(2)}) collective-permute-start(f32[64,256,16]{1,2,0:T(8,128)S(1)} %fusion.35), channel_id=1, source_target_pairs={{1,0},{2,1},{3,2},{5,4},{6,5},{7,6}} | collective-permute-start | bytes 3145736 | tf_op jit(solution)/shard_map/ppermute | solution.py:28
  39.4 51.0 %copy-start.1 = (f32[64,256,16]{1,2,0:T(8,128)S(1)}, f32[64,256,16]{1,2,0:T(8,128)}, u32[]{:S(2)}) copy-start(f32[64,256,16]{1,2,0:T(8,128)} %param.6) | copy-start | bytes 3145732
  39.4 51.0 %copy-start.2 = (bf16[16,1152]{1,0:T(8,128)(2,1)S(1)}, bf16[16,1152]{1,0:T(8,128)(2,1)}, u32[]{:S(2)}) copy-start(bf16[16,1152]{1,0:T(8,128)(2,1)} %param.7) | copy-start | bytes 110596
  39.4 17.2 %collective-permute-start.1 = (f32[64,256,16]{1,2,0:T(8,128)S(1)}, f32[64,256,16]{1,2,0:T(8,128)S(1)}, u32[]{:S(2)}, u32[]{:S(2)}) collective-permute-start(f32[64,256,16]{1,2,0:T(8,128)S(1)} %add_multiply_fusion.3), channel_id=1, source_target_pairs={{0,1},{1,2},{2,3},{4,5},{5,6},{6,7}} | collective-permute-start | bytes 3145736 | tf_op jit(solution)/shard_map/ppermute | solution.py:36
  56.8 33.6 %collective-permute-start.2 = (f32[64,256,16]{1,2,0:T(8,128)S(1)}, f32[64,256,16]{1,2,0:T(8,128)}, u32[]{:S(2)}, u32[]{:S(2)}) collective-permute-start(f32[64,256,16]{1,2,0:T(8,128)S(1)} %add.147), channel_id=1, source_target_pairs={{0,2},{1,3},{4,6},{5,7}} | collective-permute-start | bytes 3145736 | tf_op jit(solution)/shard_map/ppermute | solution.py:36
  124.8 4.5 %collective-permute-start.3 = (f32[64,256,16]{1,2,0:T(8,128)}, f32[64,256,16]{1,2,0:T(8,128)S(1)}, u32[]{:S(2)}, u32[]{:S(2)}) collective-permute-start(f32[64,256,16]{1,2,0:T(8,128)} %fusion.34), channel_id=1, source_target_pairs={{1,0},{2,1},{3,2},{5,4},{6,5},{7,6}} | collective-permute-start | bytes 3145736 | tf_op jit(solution)/shard_map/ppermute | solution.py:28
  130.8 16.6 %collective-permute-start.4 = (f32[64,256,16]{1,2,0:T(8,128)S(1)}, f32[64,256,16]{1,2,0:T(8,128)S(1)}, u32[]{:S(2)}, u32[]{:S(2)}) collective-permute-start(f32[64,256,16]{1,2,0:T(8,128)S(1)} %add_multiply_fusion.2), channel_id=1, source_target_pairs={{0,1},{1,2},{2,3},{4,5},{5,6},{6,7}} | collective-permute-start | bytes 3145736 | tf_op jit(solution)/shard_map/ppermute | solution.py:36
  147.6 33.6 %collective-permute-start.5 = (f32[64,256,16]{1,2,0:T(8,128)S(1)}, f32[64,256,16]{1,2,0:T(8,128)}, u32[]{:S(2)}, u32[]{:S(2)}) collective-permute-start(f32[64,256,16]{1,2,0:T(8,128)S(1)} %add.154), channel_id=1, source_target_pairs={{0,2},{1,3},{4,6},{5,7}} | collective-permute-start | bytes 3145736 | tf_op jit(solution)/shard_map/ppermute | solution.py:36
  215.5 4.5 %collective-permute-start.6 = (f32[64,256,16]{1,2,0:T(8,128)}, f32[64,256,16]{1,2,0:T(8,128)S(1)}, u32[]{:S(2)}, u32[]{:S(2)}) collective-permute-start(f32[64,256,16]{1,2,0:T(8,128)} %fusion.33), channel_id=1, source_target_pairs={{1,0},{2,1},{3,2},{5,4},{6,5},{7,6}} | collective-permute-start | bytes 3145736 | tf_op jit(solution)/shard_map/ppermute | solution.py:28
  221.6 16.6 %collective-permute-start.7 = (f32[64,256,16]{1,2,0:T(8,128)S(1)}, f32[64,256,16]{1,2,0:T(8,128)S(1)}, u32[]{:S(2)}, u32[]{:S(2)}) collective-permute-start(f32[64,256,16]{1,2,0:T(8,128)S(1)} %add_multiply_fusion.1), channel_id=1, source_target_pairs={{0,1},{1,2},{2,3},{4,5},{5,6},{6,7}} | collective-permute-start | bytes 3145736 | tf_op jit(solution)/shard_map/ppermute | solution.py:36
  238.4 33.6 %collective-permute-start.8 = (f32[64,256,16]{1,2,0:T(8,128)S(1)}, f32[64,256,16]{1,2,0:T(8,128)}, u32[]{:S(2)}, u32[]{:S(2)}) collective-permute-start(f32[64,256,16]{1,2,0:T(8,128)S(1)} %add.161), channel_id=1, source_target_pairs={{0,2},{1,3},{4,6},{5,7}} | collective-permute-start | bytes 3145736 | tf_op jit(solution)/shard_map/ppermute | solution.py:36
  306.3 4.5 %collective-permute-start.9 = (f32[64,256,16]{1,2,0:T(8,128)}, f32[64,256,16]{1,2,0:T(8,128)S(1)}, u32[]{:S(2)}, u32[]{:S(2)}) collective-permute-start(f32[64,256,16]{1,2,0:T(8,128)} %fusion.32), channel_id=1, source_target_pairs={{1,0},{2,1},{3,2},{5,4},{6,5},{7,6}} | collective-permute-start | bytes 3145736 | tf_op jit(solution)/shard_map/ppermute | solution.py:28
  312.3 16.6 %collective-permute-start.10 = (f32[64,256,16]{1,2,0:T(8,128)S(1)}, f32[64,256,16]{1,2,0:T(8,128)S(1)}, u32[]{:S(2)}, u32[]{:S(2)}) collective-permute-start(f32[64,256,16]{1,2,0:T(8,128)S(1)} %add_multiply_fusion), channel_id=1, source_target_pairs={{0,1},{1,2},{2,3},{4,5},{5,6},{6,7}} | collective-permute-start | bytes 3145736 | tf_op jit(solution)/shard_map/ppermute | solution.py:36
  329.2 33.6 %collective-permute-start.11 = (f32[64,256,16]{1,2,0:T(8,128)S(1)}, f32[64,256,16]{1,2,0:T(8,128)S(1)}, u32[]{:S(2)}, u32[]{:S(2)}) collective-permute-start(f32[64,256,16]{1,2,0:T(8,128)S(1)} %add.168), channel_id=1, source_target_pairs={{0,2},{1,3},{4,6},{5,7}} | collective-permute-start | bytes 3145736 | tf_op jit(solution)/shard_map/ppermute | solution.py:36
where the time goes:
time: 365 us; the launch traced here: 364 us
  matrix products  136 us (37%)
  starting transfers between devices  121 us (33%)
  waiting for transfers between devices  97.8 us (27%)
  other arithmetic  7.69 us (2%)
    dot_general x4, matrix products, drift_block(): jnp.einsum('kbnd,dc->kbnc', hidden_act.astype(jnp.bfloat16), w_out, prefe...  136 us
    ppermute x8, starting transfers between devices, local(): lax.ppermute(inclusive, 'time', [(source, source + distance) for source i...  116 us
    ppermute x8, waiting for transfers between devices, local(): lax.ppermute(inclusive, 'time', [(source, source + distance) for source i...  85.1 us
    ppermute x4, waiting for transfers between devices, local(): next_first = lax.ppermute(drifts[0], 'time', from_next)  12.7 us
  transfers between devices with their start and end apart: 12, of which 12 were waited for; matrix products, arithmetic and copies ran while one was open for 0% of the time, Pallas kernels for 0%

commit v1 on v0

v1 whole, which is shorter than its diff:
```python
import functools

import jax
import jax.numpy as jnp
from jax import lax
from jax.experimental import pallas as pl
from jax.experimental.pallas import tpu as pltpu
from jax.sharding import PartitionSpec as P

SWEEPS = 4
N_TIME = 4
CH = 16
TOK = 256
HIDDEN = 1152
BLOCK = 384
LAG = 2
GROUP = 2
GROUP_A = 4
DEPTH = 10 * CH
SQRT_2_PI = 0.7978845608028654
LINEAR = 2.0 * SQRT_2_PI
CUBIC = 8.0 * 0.044715 * SQRT_2_PI
MESH = pl.DeviceIdType.MESH
UP = 2.0**64
DOWN = 2.0**-64
SPLIT = 2.0**32


def modulated_weights(w_in, scale, shift):
    half = 0.5 * (1.0 + scale.astype(jnp.float32))
    w = w_in.astype(jnp.float32)
    w_down = w * DOWN
    low = w * half
    middle = w_down * half
    high = w_down * (half * DOWN)
    in_high = jnp.abs(high) >= SPLIT
    in_middle = jnp.logical_and(jnp.abs(middle) >= SPLIT, jnp.logical_not(in_high))
    in_low = jnp.logical_not(jnp.logical_or(in_middle, in_high))
    rows = []
    for chosen, value in ((in_low, low), (in_middle, middle), (in_high, high)):
        rest = jnp.where(chosen, value, 0.0)
        for _ in range(3):
            part = rest.astype(jnp.bfloat16)
            rest = rest - part.astype(jnp.float32)
            rows.append(part)
    first_row = lax.broadcasted_iota(jnp.int32, (CH, HIDDEN), 0) == 0
    half_shift = jnp.broadcast_to(0.5 * shift.astype(jnp.float32), (CH, HIDDEN))
    rows.append(jnp.where(first_row, half_shift, 0.0).astype(jnp.bfloat16))
    return jnp.concatenate(rows, axis=0).T


def first_rhs(latent, ones):
    top = float(jnp.finfo(jnp.bfloat16).max)
    x = latent.astype(jnp.bfloat16)
    up = jnp.clip(x * UP, -top, top)
    up_up = jnp.clip(up * UP, -top, top)
    return jnp.concatenate([x, x, x, up, up, up, up_up, up_up, up_up, ones], axis=0)


def activation(half_pre):
    cubic = half_pre * (half_pre * half_pre * CUBIC + LINEAR)
    return (half_pre * jnp.tanh(cubic) + half_pre).astype(jnp.bfloat16)


def run_evals(evals, lhs, w_out_ref, done):
    n_blocks = HIDDEN // BLOCK
    steps = [(e, b) for e in range(len(evals)) for b in range(n_blocks)]
    pre, rhs, acc = {}, {}, {}

    def issue(i):
        e, b = steps[i]
        if b == 0:
            rhs[e] = evals[e][2]()
        pre[i] = jnp.dot(lhs(evals[e][1], b), rhs[e], preferred_element_type=jnp.float32)

    for i in range(min(LAG, len(steps))):
        issue(i)
    for i, (e, b) in enumerate(steps):
        if i + LAG < len(steps):
            issue(i + LAG)
        hidden = activation(pre.pop(i))
        part = jnp.dot(w_out_ref[:, b * BLOCK:(b + 1) * BLOCK], hidden, preferred_element_type=jnp.float32)
        acc[e] = part if b == 0 else acc[e] + part
        if b == n_blocks - 1:
            done(evals[e][0], acc.pop(e))


def kernel(n_lat, x_hbm, w_in_ref, w_out_ref, scale_ref, shift_ref, step_ref, out_hbm,
           x_own, x_all, lhs_ref, drift0, stage, scales, shifts, steps_buf,
           load_sem, pass_sem, own_sem, par_send, par_recv, send_sem, recv_sem):
    me = lax.axis_index("time")
    others = [lax.rem(me + k, N_TIME) for k in range(1, N_TIME)]
    n_own = n_lat // N_TIME
    n_groups = n_own // GROUP

    load = pltpu.make_async_copy(x_hbm.at[pl.ds(me * n_own, n_own)], x_own, load_sem)
    load.start()
    steps_buf[me] = jnp.full((8, 128), 0.5 * step_ref[0], jnp.float32)
    barrier = pltpu.get_barrier_semaphore()
    for peer in others:
        pl.semaphore_signal(barrier, inc=1, device_id={"time": peer}, device_id_type=MESH)

    @pl.when(me == 0)
    def _():
        pltpu.make_async_copy(x_hbm, x_all, pass_sem).start()

    scales[me] = scale_ref[...]
    shifts[me] = shift_ref[...]
    lhs_ref[me] = modulated_weights(w_in_ref[...], scale_ref[...], shift_ref[...])
    pl.semaphore_wait(barrier, N_TIME - 1)

    def param_copies(slot, peer):
        return [
            pltpu.make_async_remote_copy(
                src_ref=src, dst_ref=dst.at[slot], send_sem=par_send.at[i, peer], recv_sem=par_recv.at[i, slot],
                device_id={"time": peer}, device_id_type=MESH)
            for i, (src, dst) in enumerate(((scale_ref, scales), (shift_ref, shifts), (steps_buf.at[slot], steps_buf)))
        ]

    for peer in others:
        for copy in param_copies(me, peer):
            copy.start()
    load.wait()

    ones = (lax.broadcasted_iota(jnp.int32, (CH, TOK), 0) == 0).astype(jnp.float32).astype(jnp.bfloat16)

    def lhs(timestep, block):
        return lhs_ref[timestep, block * BLOCK:(block + 1) * BLOCK, :]

    def own_pass(trip, carry):
        base = trip * GROUP_A
        evals = [(base + g, me, functools.partial(lambda i: first_rhs(x_own[i], ones), base + g)) for g in range(GROUP_A)]

        def done(i, drift):
            drift0[me, i] = drift

        run_evals(evals, lhs, w_out_ref, done)
        return carry

    lax.fori_loop(0, n_own // GROUP_A, own_pass, 0)

    @pl.when(me == 0)
    def _():
        pltpu.make_async_copy(x_hbm, x_all, pass_sem).wait()
        pltpu.make_async_copy(x_all, out_hbm, pass_sem).start()

    for peer in others:
        for copy in param_copies(peer, peer):
            copy.wait_recv()
    for peer in others:
        lhs_ref[peer] = modulated_weights(w_in_ref[...], scales[peer], shifts[peer])
    half_step = [steps_buf[j, 0:1, 0:1] for j in range(N_TIME - 1)]

    def data_copy(group, slot, peer):
        rows = pl.ds(group * GROUP, GROUP)
        return pltpu.make_async_remote_copy(
            src_ref=stage.at[peer, rows], dst_ref=out_hbm.at[pl.ds(slot * n_own + group * GROUP, GROUP)],
            send_sem=send_sem.at[group, peer], recv_sem=recv_sem.at[group, slot],
            device_id={"time": peer}, device_id_type=MESH)

    def own_copy(group):
        return pltpu.make_async_copy(stage.at[me, pl.ds(group * GROUP, GROUP)],
                                     out_hbm.at[pl.ds(me * n_own + group * GROUP, GROUP)], own_sem.at[group])

    def sweeps(group, carry):
        base = group * GROUP
        x0 = [x_own[base + g] for g in range(GROUP)]
        drifts = {}
        evals = []
        rhs0 = {}

        def start_rhs(g):
            if g not in rhs0:
                rhs0[g] = first_rhs(x0[g], ones)
            return rhs0[g]

        def latent(sweep, j, g):
            total = x0[g]
            for i in range(j):
                total = total + half_step[i] * (drifts[sweep, i, g] + drifts[sweep, i + 1, g])
            return total

        for k in range(N_TIME - 1):
            for g in range(GROUP):
                evals.append((("first", k, g), others[k], functools.partial(start_rhs, g)))
        for sweep in range(1, SWEEPS):
            for g in range(GROUP):
                for j in range(1, N_TIME):
                    evals.append(((sweep, j, g), j, functools.partial(
                        lambda s, j, g: first_rhs(latent(s - 1, j, g), ones), sweep, j, g)))

        def done(key, drift):
            if key[0] == "first":
                _, k, g = key
                drift0[others[k], base + g] = drift
                if k == N_TIME - 2:
                    for j in range(N_TIME):
                        drifts[0, j, g] = drift0[j, base + g]
                        if j == 0:
                            for sweep in range(1, SWEEPS):
                                drifts[sweep, 0, g] = drifts[0, 0, g]
            else:
                sweep, j, g = key
                drifts[sweep, j, g] = drift
                if sweep == SWEEPS - 1:
                    stage[j, base + g] = latent(sweep, j, g)

        run_evals(evals, lhs, w_out_ref, done)
        for peer in others:
            @pl.when(peer != 0)
            def _(peer=peer):
                data_copy(group, me, peer).start()

        @pl.when(me != 0)
        def _():
            own_copy(group).start()

        return carry

    lax.fori_loop(0, n_groups, sweeps, 0)

    for peer in others:
        for copy in param_copies(me, peer):
            copy.wait_send()

    @pl.when(me == 0)
    def _():
        pltpu.make_async_copy(x_all, out_hbm, pass_sem).wait()

    def finish(group, carry):
        for peer in others:
            @pl.when(peer != 0)
            def _(peer=peer):
                data_copy(group, me, peer).wait_send()

        @pl.when(me != 0)
        def _():
            own_copy(group).wait()
            for peer in others:
                data_copy(group, peer, peer).wait_recv()

        return carry

    lax.fori_loop(0, n_groups, finish, 0)


def solution(mesh):
    def local(x_init, w_in, w_out, mod_scale, mod_shift, step_size):
        n_lat = x_init.shape[0]
        n_own = n_lat // N_TIME
        n_groups = n_own // GROUP
        vmem = pl.BlockSpec(memory_space=pltpu.VMEM)
        out = pl.pallas_call(
            functools.partial(kernel, n_lat),
            out_shape=jax.ShapeDtypeStruct((n_lat, CH, TOK), jnp.float32),
            in_specs=[pl.BlockSpec(memory_space=pl.ANY), vmem, vmem, vmem, vmem, pl.BlockSpec(memory_space=pltpu.SMEM)],
            out_specs=pl.BlockSpec(memory_space=pl.ANY),
            scratch_shapes=[
                pltpu.VMEM((n_own, CH, TOK), jnp.float32),
                pltpu.VMEM((n_lat, CH, TOK), jnp.float32),
                pltpu.VMEM((N_TIME, HIDDEN, DEPTH), jnp.bfloat16),
                pltpu.VMEM((N_TIME, n_own, CH, TOK), jnp.float32),
                pltpu.VMEM((N_TIME, n_own, CH, TOK), jnp.float32),
                pltpu.VMEM((N_TIME, 1, HIDDEN), jnp.bfloat16),
                pltpu.VMEM((N_TIME, 1, HIDDEN), jnp.bfloat16),
                pltpu.VMEM((N_TIME, 8, 128), jnp.float32),
                pltpu.SemaphoreType.DMA,
                pltpu.SemaphoreType.DMA,
                pltpu.SemaphoreType.DMA((n_groups,)),
                pltpu.SemaphoreType.DMA((3, N_TIME)),
                pltpu.SemaphoreType.DMA((3, N_TIME)),
                pltpu.SemaphoreType.DMA((n_groups, N_TIME)),
                pltpu.SemaphoreType.DMA((n_groups, N_TIME)),
            ],
            compiler_params=pltpu.CompilerParams(collective_id=0, has_side_effects=True, vmem_limit_bytes=48 * 1024 * 1024),
        )(jnp.transpose(x_init, (0, 2, 1)), w_in, w_out.T, mod_scale, mod_shift, step_size)
        return jnp.transpose(out, (0, 2, 1))[None]

    return jax.shard_map(local, mesh=mesh, in_specs=(P("data"), P(), P(), P("time"), P("time"), P("time")), out_specs=P("time", "data"), check_vma=False)
```

time: 365 us -> 81 us (0.22)
  matrix products: 136 us -> 0 us
  starting transfers between devices: 121 us -> 0 us
  waiting for transfers between devices: 97.8 us -> 0 us
  Pallas kernels: 0 us -> 75.5 us
  other arithmetic: 7.69 us -> 0 us
  local copies, waits for them, and re-layouts: 0.03 us -> 4.44 us
    dot_general x4 -> x0, matrix products: 136 us -> none  [drift_block(): jnp.einsum('kbnd,dc->kbnc', hidden_act.astype(jnp.bfloat16), w_out, prefe...]
    ppermute x12 -> x0, starting transfers between devices: 121 us -> none  [the longest x8 116 us: local(): lax.ppermute(inclusive, 'time', [(source, source + distance) for source i...]
    ppermute x12 -> x0, waiting for transfers between devices: 97.8 us -> none  [the longest x8 85.1 us: local(): lax.ppermute(inclusive, 'time', [(source, source + distance) for source i...]
    pallas_call x0 -> x1, Pallas kernels: none -> 75.5 us  [local(): pl.pallas_call(functools.partial(kernel, n_lat), out_shape=jax.ShapeDtype...]
    mul x4 -> x0, other arithmetic: 4.65 us -> none  [local(): increments = step_size[:, None, None, None] * (0.5 * (drifts + next_drifts))]
    unnamed x6 -> x11, local copies, waits for them, and re-layouts: 0.03 us -> 4.44 us
  transfers between devices with their start and end apart: 12 -> 0, of which waited for: 12 -> 0; matrix products, arithmetic and copies ran while one was open for 0% -> 0% of each run, Pallas kernels for 0% -> 0%
where the time goes in v1:
time: 81 us; the launch traced here: 80.6 us
  Pallas kernels  75.5 us (93%)
  local copies, waits for them, and re-layouts  4.44 us (5%)
    pallas_call x1, Pallas kernels, local(): pl.pallas_call(functools.partial(kernel, n_lat), out_shape=jax.ShapeDtype...  75.5 us
    unnamed x11, local copies, waits for them, and re-layouts  4.44 us

profile of v1, /device:TPU:0, one launch (start us, length us, event | category | flops | bytes accessed | tf_op | source)
XLA Modules:
  0.0 80.6 jit_solution(14939146199926670286)
XLA Ops:
  0.0 0.0 copy-start.3
  0.7 0.0 copy-done.3
  0.7 0.0 copy-start
  0.7 1.2 %copy-done = f32[64,256,16]{1,2,0:T(8,128)S(1)} copy-done((f32[64,256,16]{1,2,0:T(8,128)S(1)}, f32[64,256,16]{1,2,0:T(8,128)}, u32[]{:S(2)}) %copy-start) | copy-done | bytes 1048600
  1.9 0.0 copy-start.1
  1.9 0.8 copy-done.1
  2.7 0.0 copy-start.2
  2.7 0.8 copy-done.2
  3.5 0.0 copy-start.4
  3.5 0.7 copy-done.4
  4.1 75.5 %shard_map.64 = f32[64,16,256]{2,1,0:T(8,128)S(1)} custom-call(f32[64,16,256]{2,1,0:T(8,128)S(1)} %bitcast.6, bf16[16,1152]{1,0:T(8,128)(2,1)S(1)} %copy-done.1, bf16[16,1152]{1,0:T(8,128)(2,1)S(1)} %bitcast.7, bf16[1,1152]{1,0:T(2,128)(2,1)S(1)} %copy-done.3, bf16[1,1152]{1,0:T(2,128)(2,1)S(1)} %copy-done.4, f32[1]{0:T(128)S(6)} %copy.8.step_ref), custom_call_target="tpu_custom_call" | custom-call | tf_op jit(solution)/shard_map/pallas_call | solution.py:253
  79.7 1.0 %copy.9 = f32[1,64,256,16]{2,3,1,0:T(8,128)} copy(f32[1,64,256,16]{2,3,1,0:T(8,128)S(1)} %bitcast.5) | data formatting | bytes 2097152
Async XLA Ops:
  0.0 0.7 copy-start.3
  0.7 1.2 %copy-start = (f32[64,256,16]{1,2,0:T(8,128)S(1)}, f32[64,256,16]{1,2,0:T(8,128)}, u32[]{:S(2)}) copy-start(f32[64,256,16]{1,2,0:T(8,128)} %param.6) | copy-start | bytes 3145732
  1.9 0.8 copy-start.1
  2.7 0.8 copy-start.2
  3.5 0.7 copy-start.4

commit v2 on v1

--- a/solution.py
+++ b/solution.py
@@ -85,17 +85,22 @@
             done(evals[e][0], acc.pop(e))
 
 
-def kernel(n_lat, x_hbm, w_in_ref, w_out_ref, scale_ref, shift_ref, step_ref, out_hbm,
-           x_own, x_all, lhs_ref, drift0, stage, scales, shifts, steps_buf,
+def kernel(n_lat, x_hbm, w_in_hbm, w_out_hbm, scale_hbm, shift_hbm, step_hbm, out_hbm,
+           w_in_ref, w_out_ref, x_own, x_all, lhs_ref, drift0, stage, scales, shifts, steps_buf,
            load_sem, pass_sem, own_sem, par_send, par_recv, send_sem, recv_sem):
     me = lax.axis_index("time")
     others = [lax.rem(me + k, N_TIME) for k in range(1, N_TIME)]
     n_own = n_lat // N_TIME
     n_groups = n_own // GROUP
 
-    load = pltpu.make_async_copy(x_hbm.at[pl.ds(me * n_own, n_own)], x_own, load_sem)
-    load.start()
-    steps_buf[me] = jnp.full((8, 128), 0.5 * step_ref[0], jnp.float32)
+    loads = [
+        pltpu.make_async_copy(src, dst, load_sem.at[i])
+        for i, (src, dst) in enumerate((
+            (scale_hbm, scales.at[me]), (shift_hbm, shifts.at[me]), (step_hbm, steps_buf.at[me]),
+            (w_in_hbm, w_in_ref), (x_hbm.at[pl.ds(me * n_own, n_own)], x_own), (w_out_hbm, w_out_ref)))
+    ]
+    for load in loads:
+        load.start()
     barrier = pltpu.get_barrier_semaphore()
     for peer in others:
         pl.semaphore_signal(barrier, inc=1, device_id={"time": peer}, device_id_type=MESH)
@@ -104,23 +109,22 @@
     def _():
         pltpu.make_async_copy(x_hbm, x_all, pass_sem).start()
 
-    scales[me] = scale_ref[...]
-    shifts[me] = shift_ref[...]
-    lhs_ref[me] = modulated_weights(w_in_ref[...], scale_ref[...], shift_ref[...])
+    for load in loads:
+        load.wait()
     pl.semaphore_wait(barrier, N_TIME - 1)
 
     def param_copies(slot, peer):
         return [
             pltpu.make_async_remote_copy(
-                src_ref=src, dst_ref=dst.at[slot], send_sem=par_send.at[i, peer], recv_sem=par_recv.at[i, slot],
+                src_ref=dst.at[slot], dst_ref=dst.at[slot], send_sem=par_send.at[i, peer], recv_sem=par_recv.at[i, slot],
                 device_id={"time": peer}, device_id_type=MESH)
-            for i, (src, dst) in enumerate(((scale_ref, scales), (shift_ref, shifts), (steps_buf.at[slot], steps_buf)))
+            for i, dst in enumerate((scales, shifts, steps_buf))
         ]
 
     for peer in others:
         for copy in param_copies(me, peer):
             copy.start()
-    load.wait()
+    lhs_ref[me] = modulated_weights(w_in_ref[...], scales[me], shifts[me])
 
     ones = (lax.broadcasted_iota(jnp.int32, (CH, TOK), 0) == 0).astype(jnp.float32).astype(jnp.bfloat16)
 
@@ -149,7 +153,7 @@
             copy.wait_recv()
     for peer in others:
         lhs_ref[peer] = modulated_weights(w_in_ref[...], scales[peer], shifts[peer])
-    half_step = [steps_buf[j, 0:1, 0:1] for j in range(N_TIME - 1)]
+    half_step = [0.5 * steps_buf[j] for j in range(N_TIME - 1)]
 
     def data_copy(group, slot, peer):
         rows = pl.ds(group * GROUP, GROUP)
@@ -249,13 +253,14 @@
         n_lat = x_init.shape[0]
         n_own = n_lat // N_TIME
         n_groups = n_own // GROUP
-        vmem = pl.BlockSpec(memory_space=pltpu.VMEM)
         out = pl.pallas_call(
             functools.partial(kernel, n_lat),
             out_shape=jax.ShapeDtypeStruct((n_lat, CH, TOK), jnp.float32),
-            in_specs=[pl.BlockSpec(memory_space=pl.ANY), vmem, vmem, vmem, vmem, pl.BlockSpec(memory_space=pltpu.SMEM)],
+            in_specs=[pl.BlockSpec(memory_space=pltpu.HBM)] * 6,
             out_specs=pl.BlockSpec(memory_space=pl.ANY),
             scratch_shapes=[
+                pltpu.VMEM((CH, HIDDEN), jnp.bfloat16),
+                pltpu.VMEM((CH, HIDDEN), jnp.bfloat16),
                 pltpu.VMEM((n_own, CH, TOK), jnp.float32),
                 pltpu.VMEM((n_lat, CH, TOK), jnp.float32),
                 pltpu.VMEM((N_TIME, HIDDEN, DEPTH), jnp.bfloat16),
@@ -263,8 +268,8 @@
                 pltpu.VMEM((N_TIME, n_own, CH, TOK), jnp.float32),
                 pltpu.VMEM((N_TIME, 1, HIDDEN), jnp.bfloat16),
                 pltpu.VMEM((N_TIME, 1, HIDDEN), jnp.bfloat16),
-                pltpu.VMEM((N_TIME, 8, 128), jnp.float32),
-                pltpu.SemaphoreType.DMA,
+                pltpu.VMEM((N_TIME, 1, 1), jnp.float32),
+                pltpu.SemaphoreType.DMA((6,)),
                 pltpu.SemaphoreType.DMA,
                 pltpu.SemaphoreType.DMA((n_groups,)),
                 pltpu.SemaphoreType.DMA((3, N_TIME)),
@@ -272,8 +277,8 @@
                 pltpu.SemaphoreType.DMA((n_groups, N_TIME)),
                 pltpu.SemaphoreType.DMA((n_groups, N_TIME)),
             ],
-            compiler_params=pltpu.CompilerParams(collective_id=0, has_side_effects=True, vmem_limit_bytes=48 * 1024 * 1024),
-        )(jnp.transpose(x_init, (0, 2, 1)), w_in, w_out.T, mod_scale, mod_shift, step_size)
+            compiler_params=pltpu.CompilerParams(collective_id=0, has_side_effects=True, vmem_limit_bytes=67_043_328),
+        )(jnp.transpose(x_init, (0, 2, 1)), w_in, w_out.T, mod_scale, mod_shift, step_size[:, None])
         return jnp.transpose(out, (0, 2, 1))[None]
 
     return jax.shard_map(local, mesh=mesh, in_specs=(P("data"), P(), P(), P("time"), P("time"), P("time")), out_specs=P("time", "data"), check_vma=False)

time: 81 us -> 79.4 us (0.980)
  local copies, waits for them, and re-layouts: 4.44 us -> 2.26 us
    unnamed x11 -> x1, local copies, waits for them, and re-layouts: 4.44 us -> 2.26 us
where the time goes in v2:
time: 79.4 us; the launch traced here: 79.2 us
  Pallas kernels  76.3 us (96%)
  local copies, waits for them, and re-layouts  2.26 us (3%)
    pallas_call x1, Pallas kernels, local(): pl.pallas_call(functools.partial(kernel, n_lat), out_shape=jax.ShapeDtype...  76.3 us
    unnamed x1, local copies, waits for them, and re-layouts  2.26 us

profile of v2, /device:TPU:0, one launch (start us, length us, event | category | flops | bytes accessed | tf_op | source)
XLA Modules:
  0.0 79.2 jit_solution(9990801972631830228)
XLA Ops:
  0.7 76.3 %shard_map.64 = f32[64,16,256]{2,1,0:T(8,128)} custom-call(f32[64,16,256]{2,1,0:T(8,128)} %bitcast.8, bf16[16,1152]{1,0:T(8,128)(2,1)} %w_in_hbm.1, bf16[16,1152]{1,0:T(8,128)(2,1)} %bitcast.9, bf16[1,1152]{1,0:T(2,128)(2,1)} %scale_hbm.1, bf16[1,1152]{1,0:T(2,128)(2,1)} %shift_hbm.1, f32[1,1]{1,0:T(1,128)} %bitcast.6.step_hbm), custom_call_target="tpu_custom_call" | custom-call | tf_op jit(solution)/shard_map/pallas_call | solution.py:256
  77.0 2.3 %copy.9 = f32[1,64,256,16]{2,3,1,0:T(8,128)} copy(f32[1,64,256,16]{2,3,1,0:T(8,128)} %bitcast.7) | data formatting | bytes 2097152
